TPU v7x, 32 devices: a whole 2x2x4 slice. The times are simulated.
32 devices in a mesh: prow: 8 (over z, x), pcol: 4 (over y, core).
Axes of the slice: x: 2, y: 2, z: 4, core: 2. Of those that a mesh axis runs over, the one named last changes fastest.
Arguments:
- matrix: float32 [16384, 16384], P('prow', 'pcol'), may hold values from -6 to 6
Outputs:
- reduced: float32 [16384, 16384], P('prow', 'pcol')
- householder_coefficients: float32 [2, 8], replicated
All inputs are finite; a program needn't handle non-finite values.
Results may differ from a plain program's by a relative error of at most 0.0003.
Values sent between devices are 32-bit elements; how exact they have to be, the bound alone decides.
No kernel may reach another device: no remote copies, remote signals or barrier semaphores. Data moves between devices by JAX's collectives and lax.ppermute only.
A program may use at most 128 MiB of HBM per device.

v0:
```python
import jax
import jax.numpy as jnp
from jax import lax
from jax.sharding import PartitionSpec as P

NB = 8


epsilon = 1e-06


def from_root(x, axis, root):
    mine = lax.axis_index(axis) == root
    return lax.psum(jnp.where(mine, x, jnp.zeros_like(x)), axis)


def precise_dot(left, right):
    return jnp.dot(left, right, precision=lax.Precision.HIGHEST)


def inner_rows(left, right):
    return lax.dot_general(left, right, (((1,), (1,)), ((), ())), precision=lax.Precision.HIGHEST)


def householder(alpha_value, sumsq):
    norm_value = jnp.sqrt(sumsq + epsilon)
    signum = jnp.where(alpha_value >= 0.0, 1.0, -1.0).astype(jnp.float32)
    beta_value = -signum * norm_value
    return (beta_value, (beta_value - alpha_value) / beta_value, alpha_value - beta_value)


def per_device(matrix):
    rows_dev, cols_dev = matrix.shape
    prow_id = lax.axis_index("prow")
    pcol_id = lax.axis_index("pcol")
    row_glob = prow_id * rows_dev + jnp.arange(rows_dev, dtype=jnp.int32)
    col_glob = pcol_id * cols_dev + jnp.arange(cols_dev, dtype=jnp.int32)
    panel_index = jnp.arange(NB, dtype=jnp.int32)
    wide_index = jnp.arange(NB + 1, dtype=jnp.int32)
    held_tile = matrix
    source_side_factor_list = []
    target_side_factor_list = []
    column_owner_rank = 0 // cols_dev
    column_local_index = 0 - column_owner_rank * cols_dev
    row_root = 0 // rows_dev
    row_local = 0 - row_root * rows_dev
    col_panel = from_root(
        held_tile[:, column_local_index : column_local_index + NB + 1].T, "pcol", column_owner_rank
    )
    row_panel = from_root(held_tile[row_local : row_local + NB, :], "prow", row_root)
    sel_rows = (row_glob[None, :] == 0 + panel_index[:, None]).astype(jnp.float32)
    sel_cols = (col_glob[None, :] == 0 + wide_index[:, None]).astype(jnp.float32)
    v_rows = jnp.zeros((NB, rows_dev), jnp.float32)
    x_rows = jnp.zeros((NB, rows_dev), jnp.float32)
    y_cols = jnp.zeros((NB, cols_dev), jnp.float32)
    u_cols = jnp.zeros((NB, cols_dev), jnp.float32)
    v_panel = jnp.zeros((NB, NB), jnp.float32)
    y_panel = jnp.zeros((NB, NB + 1), jnp.float32)
    u_panel = jnp.zeros((NB, NB + 1), jnp.float32)
    diagonal_entries = []
    super_list = []
    for i in range(NB):
        column = (
            col_panel[i] - precise_dot(y_panel[:, i], v_rows) - precise_dot(u_panel[:, i], x_rows)
        )
        masked = jnp.where(row_glob >= i, column, 0.0)
        trans_part, v_coef, x_coef, col_window, col_sumsq, x_panel = lax.psum(
            (
                precise_dot(masked, held_tile),
                precise_dot(v_rows, masked),
                precise_dot(x_rows, masked),
                precise_dot(sel_rows, masked),
                jnp.sum(masked * masked),
                inner_rows(x_rows, sel_rows),
            ),
            "prow",
        )
        row_raw = row_panel[i]
        beta_left, source_side_coefficient, denom_left = householder(col_window[i], col_sumsq)
        row_eff = row_raw - precise_dot(v_panel[:, i], y_cols) - precise_dot(x_panel[:, i], u_cols)
        transposed = (
            trans_part
            - precise_dot(v_coef, y_cols)
            - precise_dot(x_coef, u_cols)
            - beta_left * row_eff
        ) / denom_left
        y_new = jnp.where(col_glob > i, source_side_coefficient * transposed, 0.0)
        v_new = (masked - beta_left * (row_glob == i).astype(jnp.float32)) / denom_left
        v_panel = v_panel.at[i].set(
            (col_window - beta_left * (panel_index == i).astype(jnp.float32)) / denom_left
        )
        v_rows = v_rows.at[i].set(v_new)
        y_cols = y_cols.at[i].set(y_new)
        row_new = row_eff - y_new
        row_masked = jnp.where(col_glob >= i + 1, row_new, 0.0)
        prod_part, y_coef, u_coef, row_window, row_sumsq, y_panel = lax.psum(
            (
                precise_dot(held_tile, row_masked),
                precise_dot(y_cols, row_masked),
                precise_dot(u_cols, row_masked),
                precise_dot(sel_cols, row_masked),
                jnp.sum(row_masked * row_masked),
                inner_rows(y_cols, sel_cols),
            ),
            "pcol",
        )
        right_reflector_beta, target_side_coefficient, denom_right = householder(
            row_window[i + 1], row_sumsq
        )
        column_next = (
            col_panel[i + 1]
            - precise_dot(y_panel[:, i + 1], v_rows)
            - precise_dot(u_panel[:, i + 1], x_rows)
        )
        product = (
            prod_part
            - precise_dot(y_coef, v_rows)
            - precise_dot(u_coef, x_rows)
            - right_reflector_beta * column_next
        ) / denom_right
        x_new = jnp.where(row_glob > i, target_side_coefficient * product, 0.0)
        u_new = (
            row_masked - right_reflector_beta * (col_glob == i + 1).astype(jnp.float32)
        ) / denom_right
        u_panel = u_panel.at[i].set(
            (row_window - right_reflector_beta * (wide_index == i + 1).astype(jnp.float32))
            / denom_right
        )
        x_rows = x_rows.at[i].set(x_new)
        u_cols = u_cols.at[i].set(u_new)
        diagonal_entries.append(beta_left)
        super_list.append(right_reflector_beta)
        source_side_factor_list.append(source_side_coefficient)
        target_side_factor_list.append(target_side_coefficient)
    stack_left = jnp.concatenate([v_rows, x_rows], axis=0)
    stack_right = jnp.concatenate([y_cols, u_cols], axis=0)
    updated = held_tile - lax.dot_general(
        stack_left, stack_right, (((0,), (0,)), ((), ())), precision=lax.Precision.HIGHEST
    )
    col_slice = updated[:, column_local_index : column_local_index + NB]
    col_keep = jnp.logical_and(pcol_id == column_owner_rank, row_glob >= NB)[:, None]
    updated = updated.at[:, column_local_index : column_local_index + NB].set(
        jnp.where(col_keep, v_rows.T, col_slice)
    )
    row_slice = updated[row_local : row_local + NB, :]
    panel_rows_glob = (0 + panel_index)[:, None]
    col_g = col_glob[None, :]
    v_window = jnp.where(panel_index[None, :] < panel_index[:, None], v_panel.T, 0.0)
    v_part = precise_dot(v_window, sel_cols[:NB])
    diag_arr = jnp.stack(diagonal_entries)[:, None]
    super_arr = jnp.stack(super_list)[:, None]
    panel_values = jnp.where(
        col_g < 0,
        row_slice,
        jnp.where(
            col_g < panel_rows_glob,
            v_part,
            jnp.where(
                col_g == panel_rows_glob,
                diag_arr,
                jnp.where(col_g == panel_rows_glob + 1, super_arr, u_cols),
            ),
        ),
    )
    row_final = jnp.where(prow_id == row_root, panel_values, row_slice)
    held_tile = updated.at[row_local : row_local + NB, :].set(row_final)
    householder_coefficients = jnp.stack(
        [jnp.stack(source_side_factor_list), jnp.stack(target_side_factor_list)]
    )
    return (held_tile, householder_coefficients)


def solution(mesh):
    in_specs = (P("prow", "pcol"),)
    out_specs = (P("prow", "pcol"), P())
    return jax.shard_map(
        per_device, mesh=mesh, in_specs=in_specs, out_specs=out_specs, check_vma=False
    )
```

profile of v0, /device:TPU:0, one launch (start us, length us, event | category | flops | bytes accessed | tf_op | source)
XLA Modules:
  0.0 1049.0 jit_solution(7705097731152169826)
XLA Ops:
  14.8 35.1 %all-reduce.25.cloned.1.call-done = f32[9,2048]{0,1:T(8,128)} async-done(((f32[9,2048]{0,1:T(8,128)}), f32[9,2048]{0,1:T(8,128)}) %all-reduce.25.cloned.1.call-update) | async-done | bytes 73744 | tf_op jit(solution)/shard_map/psum | solution.py:14
  60.9 19.6 %fusion.321 = f32[1,4096]{1,0:T(1,128)S(1)} fusion(f32[2048,1]{0,1:T(1,128)S(1)} %bitcast.809, f32[2048,4096]{1,0:T(8,128)} %param.99), kind=kOutput, calls=%fused_computation.530 | convolution fusion | flops 100663296 | bytes 33579008 | tf_op jit(solution)/shard_map/dot_general | solution.py:18
  80.7 38.6 %all-reduce.13 = (f32[8]{0:T(128)S(1)}, f32[4096]{0:T(1024)S(1)}, f32[8]{0:T(128)S(1)}, f32[]{:T(128)}, f32[8,8]{1,0:T(8,128)S(1)}) all-reduce(f32[8]{0:T(128)S(1)} %convolution_bitcast_fusion.45, f32[4096]{0:T(1024)S(1)} %bitcast.818, f32[8]{0:T(128)S(1)} %convolution_bitcast_fusion.46, ...), channel_id=1, replica_groups=mesh['prow'=8,'pcol'=4] {'prow'}, use_global_device_ids=true, to_apply=%region_5.6 | all-reduce | flops 4177 | bytes 33416 | tf_op jit(solution)/shard_map/psum | solution.py:67
  127.5 30.7 %fusion.322 = f32[1,2048]{1,0:T(1,128)S(1)} fusion(f32[4096,1]{0,1:T(1,128)S(1)} %bitcast.802, f32[2048,4096]{1,0:T(8,128)} %param.99), kind=kOutput, calls=%fused_computation.531 | convolution fusion | flops 100663296 | bytes 33579008 | tf_op jit(solution)/shard_map/dot_general | solution.py:18
  197.5 36.5 %all-reduce.12 = (f32[8]{0:T(128)S(1)}, f32[4096]{0:T(1024)S(1)}, f32[8]{0:T(128)S(1)}, f32[8]{0:T(128)S(1)}, f32[]{:T(128)}, /*index=5*/f32[8,8]{1,0:T(8,128)S(1)}) all-reduce(f32[8]{0:T(128)S(1)} %convolution_bitcast_fusion.40, f32[4096]{0:T(1024)S(1)} %bitcast.813, ...), channel_id=1, replica_groups=mesh['prow'=8,'pcol'=4] {'prow'}, use_global_device_ids=true, to_apply=%region_20.21 | all-reduce | flops 4185 | bytes 33480 | tf_op jit(solution)/shard_map/psum | solution.py:67
  240.9 30.7 %fusion.324 = f32[1,2048]{1,0:T(1,128)S(1)} fusion(f32[4096,1]{0,1:T(1,128)S(1)} %bitcast.774, f32[2048,4096]{1,0:T(8,128)} %param.99), kind=kOutput, calls=%fused_computation.533 | convolution fusion | flops 100663296 | bytes 33579008 | tf_op jit(solution)/shard_map/dot_general | solution.py:18
  296.4 19.5 %fusion.325 = f32[1,4096]{1,0:T(1,128)S(1)} fusion(f32[2048,1]{0,1:T(1,128)S(1)} %bitcast.777, f32[2048,4096]{1,0:T(8,128)} %param.99), kind=kOutput, calls=%fused_computation.534 | convolution fusion | flops 100663296 | bytes 33579008 | tf_op jit(solution)/shard_map/dot_general | solution.py:18
  316.6 34.1 %all-reduce.11 = (f32[8]{0:T(128)S(1)}, f32[4096]{0:T(1024)S(1)}, f32[8]{0:T(128)S(1)}, f32[8]{0:T(128)S(1)}, f32[]{:T(128)}, /*index=5*/f32[8,8]{1,0:T(8,128)S(1)}) all-reduce(f32[8]{0:T(128)S(1)} %convolution_bitcast_fusion.35, f32[4096]{0:T(1024)S(1)} %bitcast.811, ...), channel_id=1, replica_groups=mesh['prow'=8,'pcol'=4] {'prow'}, use_global_device_ids=true, to_apply=%region_34.35 | all-reduce | flops 4185 | bytes 33480 | tf_op jit(solution)/shard_map/psum | solution.py:67
  358.3 30.7 %fusion.326 = f32[1,2048]{1,0:T(1,128)S(1)} fusion(f32[4096,1]{0,1:T(1,128)S(1)} %bitcast.754, f32[2048,4096]{1,0:T(8,128)} %param.99), kind=kOutput, calls=%fused_computation.535 | convolution fusion | flops 100663296 | bytes 33579008 | tf_op jit(solution)/shard_map/dot_general | solution.py:18
  413.6 19.5 %fusion.327 = f32[1,4096]{1,0:T(1,128)S(1)} fusion(f32[2048,1]{0,1:T(1,128)S(1)} %bitcast.785, f32[2048,4096]{1,0:T(8,128)} %param.99), kind=kOutput, calls=%fused_computation.536 | convolution fusion | flops 100663296 | bytes 33579008 | tf_op jit(solution)/shard_map/dot_general | solution.py:18
  433.8 34.1 %all-reduce.10 = (f32[8]{0:T(128)S(1)}, f32[4096]{0:T(1024)S(1)}, f32[8]{0:T(128)S(1)}, f32[8]{0:T(128)S(1)}, f32[]{:T(128)}, /*index=5*/f32[8,8]{1,0:T(8,128)S(1)}) all-reduce(f32[8]{0:T(128)S(1)} %convolution_bitcast_fusion.30, f32[4096]{0:T(1024)S(1)} %bitcast.814, ...), channel_id=1, replica_groups=mesh['prow'=8,'pcol'=4] {'prow'}, use_global_device_ids=true, to_apply=%region_48.49 | all-reduce | flops 4185 | bytes 33480 | tf_op jit(solution)/shard_map/psum | solution.py:67
  475.6 30.7 %fusion.328 = f32[1,2048]{1,0:T(1,128)S(1)} fusion(f32[4096,1]{0,1:T(1,128)S(1)} %bitcast.758, f32[2048,4096]{1,0:T(8,128)} %param.99), kind=kOutput, calls=%fused_computation.537 | convolution fusion | flops 100663296 | bytes 33579008 | tf_op jit(solution)/shard_map/dot_general | solution.py:18
  530.8 19.5 %fusion.329 = f32[1,4096]{1,0:T(1,128)S(1)} fusion(f32[2048,1]{0,1:T(1,128)S(1)} %bitcast.789, f32[2048,4096]{1,0:T(8,128)} %param.99), kind=kOutput, calls=%fused_computation.538 | convolution fusion | flops 100663296 | bytes 33579008 | tf_op jit(solution)/shard_map/dot_general | solution.py:18
  550.9 34.1 %all-reduce.9 = (f32[8]{0:T(128)S(1)}, f32[4096]{0:T(1024)S(1)}, f32[8]{0:T(128)S(1)}, f32[8]{0:T(128)S(1)}, f32[]{:T(128)}, /*index=5*/f32[8,8]{1,0:T(8,128)S(1)}) all-reduce(f32[8]{0:T(128)S(1)} %convolution_bitcast_fusion.25, f32[4096]{0:T(1024)S(1)} %bitcast.815, ...), channel_id=1, replica_groups=mesh['prow'=8,'pcol'=4] {'prow'}, use_global_device_ids=true, to_apply=%region_62.63 | all-reduce | flops 4185 | bytes 33480 | tf_op jit(solution)/shard_map/psum | solution.py:67
  592.4 30.7 %fusion.330 = f32[1,2048]{1,0:T(1,128)S(1)} fusion(f32[4096,1]{0,1:T(1,128)S(1)} %bitcast.762, f32[2048,4096]{1,0:T(8,128)} %param.99), kind=kOutput, calls=%fused_computation.539 | convolution fusion | flops 100663296 | bytes 33579008 | tf_op jit(solution)/shard_map/dot_general | solution.py:18
  647.9 19.5 %fusion.331 = f32[1,4096]{1,0:T(1,128)S(1)} fusion(f32[2048,1]{0,1:T(1,128)S(1)} %bitcast.793, f32[2048,4096]{1,0:T(8,128)} %param.99), kind=kOutput, calls=%fused_computation.540 | convolution fusion | flops 100663296 | bytes 33579008 | tf_op jit(solution)/shard_map/dot_general | solution.py:18
  668.1 34.1 %all-reduce.8 = (f32[8]{0:T(128)S(1)}, f32[4096]{0:T(1024)S(1)}, f32[8]{0:T(128)S(1)}, f32[8]{0:T(128)S(1)}, f32[]{:T(128)}, /*index=5*/f32[8,8]{1,0:T(8,128)S(1)}) all-reduce(f32[8]{0:T(128)S(1)} %convolution_bitcast_fusion.20, f32[4096]{0:T(1024)S(1)} %bitcast.816, ...), channel_id=1, replica_groups=mesh['prow'=8,'pcol'=4] {'prow'}, use_global_device_ids=true, to_apply=%region_76.77 | all-reduce | flops 4185 | bytes 33480 | tf_op jit(solution)/shard_map/psum | solution.py:67
  710.1 30.7 %fusion.332 = f32[1,2048]{1,0:T(1,128)S(1)} fusion(f32[4096,1]{0,1:T(1,128)S(1)} %bitcast.766, f32[2048,4096]{1,0:T(8,128)} %param.99), kind=kOutput, calls=%fused_computation.541 | convolution fusion | flops 100663296 | bytes 33579008 | tf_op jit(solution)/shard_map/dot_general | solution.py:18
  785.5 34.1 %all-reduce.7 = (f32[8]{0:T(128)S(1)}, f32[4096]{0:T(1024)S(1)}, f32[8]{0:T(128)S(1)}, f32[8]{0:T(128)S(1)}, f32[]{:T(128)}, /*index=5*/f32[8,8]{1,0:T(8,128)S(1)}) all-reduce(f32[8]{0:T(128)S(1)} %convolution_bitcast_fusion.15, f32[4096]{0:T(1024)S(1)} %bitcast.817, ...), channel_id=1, replica_groups=mesh['prow'=8,'pcol'=4] {'prow'}, use_global_device_ids=true, to_apply=%region_90.91 | all-reduce | flops 4185 | bytes 33480 | tf_op jit(solution)/shard_map/psum | solution.py:67
  827.1 30.7 %fusion.334 = f32[1,2048]{1,0:T(1,128)S(1)} fusion(f32[4096,1]{0,1:T(1,128)S(1)} %bitcast.750, f32[2048,4096]{1,0:T(8,128)} %param.99), kind=kOutput, calls=%fused_computation.543 | convolution fusion | flops 100663296 | bytes 33579008 | tf_op jit(solution)/shard_map/dot_general | solution.py:18
  882.1 19.5 %fusion.335 = f32[1,4096]{1,0:T(1,128)S(1)} fusion(f32[2048,1]{0,1:T(1,128)S(1)} %bitcast.781, f32[2048,4096]{1,0:T(8,128)} %param.99), kind=kOutput, calls=%fused_computation.544 | convolution fusion | flops 100663296 | bytes 33579008 | tf_op jit(solution)/shard_map/dot_general | solution.py:18
  902.3 34.0 %all-reduce.6 = (f32[8]{0:T(128)S(1)}, f32[4096]{0:T(1024)S(1)}, f32[8]{0:T(128)S(1)}, f32[8]{0:T(128)S(1)}, f32[]{:T(128)}, /*index=5*/f32[8,8]{1,0:T(8,128)S(1)}) all-reduce(f32[8]{0:T(128)S(1)} %convolution_bitcast_fusion.10, f32[4096]{0:T(1024)S(1)} %bitcast.812, ...), channel_id=1, replica_groups=mesh['prow'=8,'pcol'=4] {'prow'}, use_global_device_ids=true, to_apply=%region_105.106 | all-reduce | flops 4185 | bytes 33480 | tf_op jit(solution)/shard_map/psum | solution.py:67
  943.6 30.7 %fusion.336 = f32[1,2048]{1,0:T(1,128)S(1)} fusion(f32[4096,1]{0,1:T(1,128)S(1)} %bitcast.770, f32[2048,4096]{1,0:T(8,128)} %param.99), kind=kOutput, calls=%fused_computation.545 | convolution fusion | flops 100663296 | bytes 33579008 | tf_op jit(solution)/shard_map/dot_general | solution.py:18
  997.8 32.9 %convolution_subtract_fusion = f32[2048,4096]{1,0:T(8,128)} fusion(f32[2048,4096]{1,0:T(8,128)} %param.99, f32[8,4096]{1,0:T(8,128)S(1)} %scatter.239, f32[8,4096]{1,0:T(8,128)S(1)} %scatter.235, f32[8,2048]{1,0:T(8,128)S(1)} %scatter.236, f32[8,2048]{1,0:T(8,128)S(1)} %copy.27), kind=kOutput, calls=%fused_computation | convolution fusion | flops 1619099648 | bytes 67502080 | tf_op jit(solution)/shard_map/dot_general | solution.py:137
  (333 shorter events, 282.0 us)
Async XLA Ops:
  7.2 42.8 %all-reduce.25.cloned.1.call-start = ((), (), s32[]{:S(2)}) async-start(), calls=%async_computation | async-start | bytes 2097152 | tf_op jit(solution)/shard_map/psum | solution.py:14
  9.5 114.8 %all-reduce.27.cloned.1.call-start = ((), (), s32[]{:S(2)}) async-start(), calls=%async_computation.1 | async-start | bytes 262144 | tf_op jit(solution)/shard_map/psum | solution.py:14
  882.1 114.7 %copy-start.1 = (f32[2048]{0:T(1024)S(1)}, f32[2048]{0:T(1024)}, u32[]{:S(2)}) copy-start(f32[2048]{0:T(1024)} %get-tuple-element.590) | copy-start | bytes 24580
  997.7 32.9 %copy-start.2 = (pred[2048]{0:T(1024)(128)(4,1)S(1)}, pred[2048]{0:T(1024)(128)(4,1)}, u32[]{:S(2)}) copy-start(pred[2048]{0:T(1024)(128)(4,1)} %fusion.145) | copy-start | bytes 6148
  997.8 41.9 %copy-start = (pred[9,4096]{1,0:T(8,128)(4,1)S(1)}, pred[9,4096]{1,0:T(8,128)(4,1)}, u32[]{:S(2)}) copy-start(pred[9,4096]{1,0:T(8,128)(4,1)} %iota_compare_fusion) | copy-start | bytes 110596
  997.8 41.9 %copy-start.3 = (pred[4096]{0:T(1024)(128)(4,1)S(1)}, pred[4096]{0:T(1024)(128)(4,1)}, u32[]{:S(2)}) copy-start(pred[4096]{0:T(1024)(128)(4,1)} %fusion.94) | copy-start | bytes 12292
  997.8 41.9 %copy-start.4 = (s32[8]{0:T(128)S(1)}, s32[8]{0:T(128)}, u32[]{:S(2)}) copy-start(s32[8]{0:T(128)} %iota_add_fusion.2) | copy-start | bytes 100
Sparse Core Ops, SparseCore 0:
  10.9 38.9 all-reduce.24
  53.3 71.0 all-reduce.26
where the time goes:
time: 1060 us; the launch traced here: 1050 us
  matrix products  483 us (46%)
  blocking collectives  369 us (35%)
  local copies, waits for them, and re-layouts  80.7 us (8%)
  between operations  56.4 us (5%)
  waiting for transfers between devices  38 us (4%)
  other arithmetic  21.1 us (2%)
    dot_general x134, matrix products, precise_dot(): return jnp.dot(left, right, precision=lax.Precision.HIGHEST)  447 us
    psum x8, blocking collectives, per_device(): lax.psum((precise_dot(masked, held_tile), precise_dot(v_rows, masked), pr...  280 us
    psum x8, blocking collectives, per_device(): lax.psum((precise_dot(held_tile, row_masked), precise_dot(y_cols, row_mas...  89.6 us
    psum x2, waiting for transfers between devices, from_root(): return lax.psum(jnp.where(mine, x, jnp.zeros_like(x)), axis)  38 us
    scatter x9, local copies, waits for them, and re-layouts, per_device(): v_rows = v_rows.at[i].set(v_new)  33.3 us
    dot_general x1, matrix products, per_device(): lax.dot_general(stack_left, stack_right, (((0,), (0,)), ((), ())), precis...  32.9 us
  transfers between devices with their start and end apart: 2, of which 2 were waited for; matrix products, arithmetic and copies ran while one was open for 4% of the time, Pallas kernels for 0%

commit v1 on v0

--- a/solution.py
+++ b/solution.py
@@ -1,6 +1,8 @@
 import jax
 import jax.numpy as jnp
 from jax import lax
+from jax.experimental import pallas as pl
+from jax.experimental.pallas import tpu as pltpu
 from jax.sharding import PartitionSpec as P
 
 NB = 8
@@ -10,8 +12,103 @@
 
 
 def from_root(x, axis, root):
-    mine = lax.axis_index(axis) == root
-    return lax.psum(jnp.where(mine, x, jnp.zeros_like(x)), axis)
+    return lax.all_gather(x, axis)[root]
+
+
+def sum_parts(long, parts, axis):
+    flat = [part.reshape(-1) for part in parts]
+    count = sum(part.size for part in flat)
+    pad = jnp.zeros((-count % 128,), jnp.float32)
+    total = jnp.sum(lax.all_gather(jnp.concatenate([long, *flat, pad]), axis), axis=0)
+    outs = [total[: long.size]]
+    at = long.size
+    for part in parts:
+        outs.append(total[at : at + part.size].reshape(part.shape))
+        at += part.size
+    return outs
+
+
+def put_row(stack, i, row):
+    at = lax.broadcasted_iota(jnp.int32, stack.shape, 0) == i
+    return jnp.where(at, row[None, :], stack)
+
+
+def thirds(x):
+    high = lax.reduce_precision(x, 8, 7)
+    rest = x - high
+    middle = lax.reduce_precision(rest, 8, 7)
+    low = lax.reduce_precision(rest - middle, 8, 7)
+    return [part.astype(jnp.bfloat16) for part in (high, middle, low)]
+
+
+def pick(n, cap):
+    b = cap
+    while n % b:
+        b //= 2
+    return b
+
+def left_kernel(v_ref, a_ref, out_ref, acc_ref):
+    step = pl.program_id(0)
+    @pl.when(step == 0)
+    def _():
+        acc_ref[...] = jnp.zeros_like(acc_ref)
+    bm, cols = a_ref.shape
+    wide = jnp.concatenate([jnp.broadcast_to(v_ref[0, r:r+1, :], (128, 128)).T for r in range(bm // 128)], axis=0)
+    for c in range(0, cols, 1024):
+        acc = [acc_ref[:, c + 128*j: c + 128*(j+1)] for j in range(8)]
+        for r in range(0, bm, 8):
+            w = wide[r:r+8, :]
+            for j in range(8):
+                acc[j] = acc[j] + w * a_ref[r:r+8, c+128*j:c+128*(j+1)]
+        for j in range(8):
+            acc_ref[:, c + 128*j: c + 128*(j+1)] = acc[j]
+    @pl.when(step == pl.num_programs(0) - 1)
+    def _():
+        out_ref[...] = jnp.sum(acc_ref[...], axis=0, keepdims=True)
+
+def left_product(v, a, bm=256):
+    rows, cols = a.shape
+    bm = pick(rows, bm)
+    return pl.pallas_call(
+        left_kernel, grid=(rows // bm,),
+        in_specs=[pl.BlockSpec((1, bm // 128, 128), lambda i: (i, 0, 0)), pl.BlockSpec((bm, cols), lambda i: (i, 0))],
+        out_specs=pl.BlockSpec((1, cols), lambda i: (0, 0)),
+        out_shape=jax.ShapeDtypeStruct((1, cols), jnp.float32),
+        scratch_shapes=[pltpu.VMEM((8, cols), jnp.float32)],
+        compiler_params=pltpu.CompilerParams(dimension_semantics=("arbitrary",), vmem_limit_bytes=48*1024*1024),
+        name="left_product",
+    )(v.reshape(rows // bm, bm // 128, 128), a)[0]
+
+def right_kernel(u_ref, a_ref, out_ref):
+    bm, cols = a_ref.shape
+    n = cols // 128
+    for g in range(bm // 128):
+        part = None
+        accs = [None] * 16
+        for c0 in range(0, n, 16):
+            us = [jnp.broadcast_to(u_ref[0:1, 128*c:128*(c+1)], (8, 128)) for c in range(c0, min(c0+16, n))]
+            for q in range(16):
+                r = g*128 + q*8
+                acc = accs[q]
+                for k, w in enumerate(us):
+                    c = c0 + k
+                    t = w * a_ref[r:r+8, 128*c:128*(c+1)]
+                    acc = t if acc is None else acc + t
+                accs[q] = acc
+        full = jnp.concatenate(accs, axis=0)
+        out_ref[0, g:g+1, :] = jnp.sum(full.T, axis=0, keepdims=True)
+
+def right_product(u, a, bm=256):
+    rows, cols = a.shape
+    bm = pick(rows, bm)
+    return pl.pallas_call(
+        right_kernel, grid=(rows // bm,),
+        in_specs=[pl.BlockSpec((1, cols), lambda i: (0, 0)), pl.BlockSpec((bm, cols), lambda i: (i, 0))],
+        out_specs=pl.BlockSpec((1, bm // 128, 128), lambda i: (i, 0, 0)),
+        out_shape=jax.ShapeDtypeStruct((rows // bm, bm // 128, 128), jnp.float32),
+        compiler_params=pltpu.CompilerParams(dimension_semantics=("arbitrary",), vmem_limit_bytes=48*1024*1024),
+        name="right_product",
+    )(u[None], a).reshape(rows)
 
 
 def precise_dot(left, right):
@@ -47,7 +144,13 @@
     col_panel = from_root(
         held_tile[:, column_local_index : column_local_index + NB + 1].T, "pcol", column_owner_rank
     )
-    row_panel = from_root(held_tile[row_local : row_local + NB, :], "prow", row_root)
+    half = NB // 2
+    row_panel = jnp.concatenate(
+        [
+            from_root(held_tile[row_local + at : row_local + at + half, :], "prow", row_root)
+            for at in (0, half)
+        ]
+    )
     sel_rows = (row_glob[None, :] == 0 + panel_index[:, None]).astype(jnp.float32)
     sel_cols = (col_glob[None, :] == 0 + wide_index[:, None]).astype(jnp.float32)
     v_rows = jnp.zeros((NB, rows_dev), jnp.float32)
@@ -64,9 +167,9 @@
             col_panel[i] - precise_dot(y_panel[:, i], v_rows) - precise_dot(u_panel[:, i], x_rows)
         )
         masked = jnp.where(row_glob >= i, column, 0.0)
-        trans_part, v_coef, x_coef, col_window, col_sumsq, x_panel = lax.psum(
+        trans_part, v_coef, x_coef, col_window, col_sumsq, x_panel = sum_parts(
+            left_product(masked, held_tile),
             (
-                precise_dot(masked, held_tile),
                 precise_dot(v_rows, masked),
                 precise_dot(x_rows, masked),
                 precise_dot(sel_rows, masked),
@@ -86,16 +189,18 @@
         ) / denom_left
         y_new = jnp.where(col_glob > i, source_side_coefficient * transposed, 0.0)
         v_new = (masked - beta_left * (row_glob == i).astype(jnp.float32)) / denom_left
-        v_panel = v_panel.at[i].set(
-            (col_window - beta_left * (panel_index == i).astype(jnp.float32)) / denom_left
-        )
-        v_rows = v_rows.at[i].set(v_new)
-        y_cols = y_cols.at[i].set(y_new)
+        v_panel = put_row(
+            v_panel,
+            i,
+            (col_window - beta_left * (panel_index == i).astype(jnp.float32)) / denom_left,
+        )
+        v_rows = put_row(v_rows, i, v_new)
+        y_cols = put_row(y_cols, i, y_new)
         row_new = row_eff - y_new
         row_masked = jnp.where(col_glob >= i + 1, row_new, 0.0)
-        prod_part, y_coef, u_coef, row_window, row_sumsq, y_panel = lax.psum(
+        prod_part, y_coef, u_coef, row_window, row_sumsq, y_panel = sum_parts(
+            right_product(row_masked, held_tile),
             (
-                precise_dot(held_tile, row_masked),
                 precise_dot(y_cols, row_masked),
                 precise_dot(u_cols, row_masked),
                 precise_dot(sel_cols, row_masked),
@@ -122,20 +227,27 @@
         u_new = (
             row_masked - right_reflector_beta * (col_glob == i + 1).astype(jnp.float32)
         ) / denom_right
-        u_panel = u_panel.at[i].set(
+        u_panel = put_row(
+            u_panel,
+            i,
             (row_window - right_reflector_beta * (wide_index == i + 1).astype(jnp.float32))
-            / denom_right
-        )
-        x_rows = x_rows.at[i].set(x_new)
-        u_cols = u_cols.at[i].set(u_new)
+            / denom_right,
+        )
+        x_rows = put_row(x_rows, i, x_new)
+        u_cols = put_row(u_cols, i, u_new)
         diagonal_entries.append(beta_left)
         super_list.append(right_reflector_beta)
         source_side_factor_list.append(source_side_coefficient)
         target_side_factor_list.append(target_side_coefficient)
     stack_left = jnp.concatenate([v_rows, x_rows], axis=0)
     stack_right = jnp.concatenate([y_cols, u_cols], axis=0)
+    lh, lm, ll = thirds(stack_left)
+    rh, rm, rl = thirds(stack_right)
     updated = held_tile - lax.dot_general(
-        stack_left, stack_right, (((0,), (0,)), ((), ())), precision=lax.Precision.HIGHEST
+        jnp.concatenate([lh, lh, lm, lm, lh, ll], axis=0),
+        jnp.concatenate([rh, rm, rh, rm, rl, rh], axis=0),
+        (((0,), (0,)), ((), ())),
+        preferred_element_type=jnp.float32,
     )
     col_slice = updated[:, column_local_index : column_local_index + NB]
     col_keep = jnp.logical_and(pcol_id == column_owner_rank, row_glob >= NB)[:, None]

time: 1060 us -> 735 us (0.69)
  matrix products: 483 us -> 65.8 us
  Pallas kernels: 0 us -> 199 us
  local copies, waits for them, and re-layouts: 80.7 us -> 38.5 us
  waiting for transfers between devices: 38 us -> 0 us
  between operations: 56.4 us -> 42.8 us
  blocking collectives: 369 us -> 358 us
    dot_general x134 -> x119, matrix products: 447 us -> 36.8 us  [precise_dot(): return jnp.dot(left, right, precision=lax.Precision.HIGHEST)]
    psum x16 -> x0, blocking collectives: 369 us -> none  [the longest x8 280 us: per_device(): lax.psum((precise_dot(masked, held_tile), precise_dot(v_rows, masked), pr...]
    all_gather x0 -> x19, blocking collectives: none -> 358 us  [the longest x16 287 us: sum_parts(): lax.all_gather(jnp.concatenate([long, *flat, pad]), axis)]
    pallas_call x0 -> x16, Pallas kernels: none -> 199 us  [the longest x8 101 us: left_product(): pl.pallas_call(left_kernel, grid=(rows // bm,), in_specs=[pl.BlockSpec((1...]
    scatter x48 -> x0, local copies, waits for them, and re-layouts: 44.6 us -> none  [the longest x9 33.3 us: per_device(): v_rows = v_rows.at[i].set(v_new)]
    psum x2 -> x0, waiting for transfers between devices: 38 us -> none  [from_root(): return lax.psum(jnp.where(mine, x, jnp.zeros_like(x)), axis)]
    concatenate x0 -> x16, local copies, waits for them, and re-layouts: none -> 11.6 us  [sum_parts(): jnp.concatenate([long, *flat, pad])]
  transfers between devices with their start and end apart: 2 -> 0, of which waited for: 2 -> 0; matrix products, arithmetic and copies ran while one was open for 4% -> 0% of each run, Pallas kernels for 0% -> 0%
where the time goes in v1:
time: 735 us; the launch traced here: 725 us
  blocking collectives  358 us (49%)
  Pallas kernels  199 us (27%)
  matrix products  65.8 us (9%)
  between operations  42.8 us (6%)
  local copies, waits for them, and re-layouts  38.5 us (5%)
  other arithmetic  20.3 us (3%)
    all_gather x16, blocking collectives, sum_parts(): lax.all_gather(jnp.concatenate([long, *flat, pad]), axis)  287 us
    pallas_call x8, Pallas kernels, left_product(): pl.pallas_call(left_kernel, grid=(rows // bm,), in_specs=[pl.BlockSpec((1...  101 us
    pallas_call x8, Pallas kernels, right_product(): pl.pallas_call(right_kernel, grid=(rows // bm,), in_specs=[pl.BlockSpec((...  98.5 us
    all_gather x3, blocking collectives, from_root(): return lax.all_gather(x, axis)[root]  71 us
    dot_general x119, matrix products, precise_dot(): return jnp.dot(left, right, precision=lax.Precision.HIGHEST)  36.8 us
    dot_general x1, matrix products, per_device(): lax.dot_general(jnp.concatenate([lh, lh, lm, lm, lh, ll], axis=0), jnp.co...  24.9 us

profile of v1, /device:TPU:0, one launch (start us, length us, event | category | flops | bytes accessed | tf_op | source)
XLA Modules:
  0.0 724.7 jit_solution(7532729367083104461)
XLA Ops:
  13.0 12.6 %left_product.8 = f32[1,4096]{1,0:T(1,128)S(1)} custom-call(f32[8,2,128]{2,1,0:T(2,128)S(1)} %bitcast.606, f32[2048,4096]{1,0:T(8,128)} %a_ref.31), custom_call_target="tpu_custom_call" | custom-call | tf_op jit(solution)/shard_map/left_product/pallas_call | solution.py:72
  26.3 30.9 %all-gather.22 = f32[8,1,4224]{2,1,0:T(1,128)S(1)} all-gather(f32[1,1,4224]{2,1,0:T(1,128)S(1)} %reshape.504), channel_id=5, replica_groups=mesh['prow'=8,'pcol'=4] {'prow'}, dimensions={0}, use_global_device_ids=true | all-gather | bytes 152064 | tf_op jit(solution)/shard_map/all_gather | solution.py:22
  62.5 31.2 %all-gather.21 = f32[8,4,4096]{2,1,0:T(4,128)S(1)} all-gather(f32[1,4,4096]{2,1,0:T(4,128)S(1)} %get-tuple-element.82), channel_id=4, replica_groups=mesh['prow'=8,'pcol'=4] {'prow'}, dimensions={0}, use_global_device_ids=true | all-gather | bytes 589824 | tf_op jit(solution)/shard_map/all_gather | solution.py:15
  95.7 12.3 %right_product.8 = f32[8,2,128]{2,1,0:T(2,128)S(1)} custom-call(f32[1,4096]{1,0:T(1,128)S(1)} %bitcast.578, f32[2048,4096]{1,0:T(8,128)} %a_ref.31), custom_call_target="tpu_custom_call" | custom-call | tf_op jit(solution)/shard_map/right_product/pallas_call | solution.py:104
  120.1 12.6 %left_product.9 = f32[1,4096]{1,0:T(1,128)S(1)} custom-call(f32[8,2,128]{2,1,0:T(2,128)S(1)} %bitcast.609, f32[2048,4096]{1,0:T(8,128)} %a_ref.31), custom_call_target="tpu_custom_call" | custom-call | tf_op jit(solution)/shard_map/left_product/pallas_call | solution.py:72
  133.9 30.6 %all-gather.24 = f32[8,1,4224]{2,1,0:T(1,128)S(1)} all-gather(f32[1,1,4224]{2,1,0:T(1,128)S(1)} %reshape.508), channel_id=7, replica_groups=mesh['prow'=8,'pcol'=4] {'prow'}, dimensions={0}, use_global_device_ids=true | all-gather | bytes 152064 | tf_op jit(solution)/shard_map/all_gather | solution.py:22
  172.0 12.3 %right_product.9 = f32[8,2,128]{2,1,0:T(2,128)S(1)} custom-call(f32[1,4096]{1,0:T(1,128)S(1)} %bitcast.591, f32[2048,4096]{1,0:T(8,128)} %a_ref.31), custom_call_target="tpu_custom_call" | custom-call | tf_op jit(solution)/shard_map/right_product/pallas_call | solution.py:104
  196.5 12.6 %left_product.10 = f32[1,4096]{1,0:T(1,128)S(1)} custom-call(f32[8,2,128]{2,1,0:T(2,128)S(1)} %bitcast.613, f32[2048,4096]{1,0:T(8,128)} %a_ref.31), custom_call_target="tpu_custom_call" | custom-call | tf_op jit(solution)/shard_map/left_product/pallas_call | solution.py:72
  210.0 30.5 %all-gather.26 = f32[8,1,4224]{2,1,0:T(1,128)S(1)} all-gather(f32[1,1,4224]{2,1,0:T(1,128)S(1)} %reshape.512), channel_id=9, replica_groups=mesh['prow'=8,'pcol'=4] {'prow'}, dimensions={0}, use_global_device_ids=true | all-gather | bytes 152064 | tf_op jit(solution)/shard_map/all_gather | solution.py:22
  247.8 12.3 %right_product.10 = f32[8,2,128]{2,1,0:T(2,128)S(1)} custom-call(f32[1,4096]{1,0:T(1,128)S(1)} %bitcast.583, f32[2048,4096]{1,0:T(8,128)} %a_ref.31), custom_call_target="tpu_custom_call" | custom-call | tf_op jit(solution)/shard_map/right_product/pallas_call | solution.py:104
  273.0 12.6 %left_product.11 = f32[1,4096]{1,0:T(1,128)S(1)} custom-call(f32[8,2,128]{2,1,0:T(2,128)S(1)} %bitcast.617, f32[2048,4096]{1,0:T(8,128)} %a_ref.31), custom_call_target="tpu_custom_call" | custom-call | tf_op jit(solution)/shard_map/left_product/pallas_call | solution.py:72
  286.5 30.5 %all-gather.28 = f32[8,1,4224]{2,1,0:T(1,128)S(1)} all-gather(f32[1,1,4224]{2,1,0:T(1,128)S(1)} %reshape.516), channel_id=11, replica_groups=mesh['prow'=8,'pcol'=4] {'prow'}, dimensions={0}, use_global_device_ids=true | all-gather | bytes 152064 | tf_op jit(solution)/shard_map/all_gather | solution.py:22
  349.0 12.6 %left_product.12 = f32[1,4096]{1,0:T(1,128)S(1)} custom-call(f32[8,2,128]{2,1,0:T(2,128)S(1)} %bitcast.621, f32[2048,4096]{1,0:T(8,128)} %a_ref.31), custom_call_target="tpu_custom_call" | custom-call | tf_op jit(solution)/shard_map/left_product/pallas_call | solution.py:72
  362.4 30.5 %all-gather.30 = f32[8,1,4224]{2,1,0:T(1,128)S(1)} all-gather(f32[1,1,4224]{2,1,0:T(1,128)S(1)} %reshape.520), channel_id=13, replica_groups=mesh['prow'=8,'pcol'=4] {'prow'}, dimensions={0}, use_global_device_ids=true | all-gather | bytes 152064 | tf_op jit(solution)/shard_map/all_gather | solution.py:22
  398.0 31.2 %all-gather.20 = f32[8,4,4096]{2,1,0:T(4,128)S(1)} all-gather(f32[1,4,4096]{2,1,0:T(4,128)S(1)} %get-tuple-element.81), channel_id=3, replica_groups=mesh['prow'=8,'pcol'=4] {'prow'}, dimensions={0}, use_global_device_ids=true | all-gather | bytes 589824 | tf_op jit(solution)/shard_map/all_gather | solution.py:15
  456.1 12.6 %left_product.13 = f32[1,4096]{1,0:T(1,128)S(1)} custom-call(f32[8,2,128]{2,1,0:T(2,128)S(1)} %bitcast.625, f32[2048,4096]{1,0:T(8,128)} %a_ref.31), custom_call_target="tpu_custom_call" | custom-call | tf_op jit(solution)/shard_map/left_product/pallas_call | solution.py:72
  469.5 30.9 %all-gather.32 = f32[8,1,4224]{2,1,0:T(1,128)S(1)} all-gather(f32[1,1,4224]{2,1,0:T(1,128)S(1)} %reshape.524), channel_id=15, replica_groups=mesh['prow'=8,'pcol'=4] {'prow'}, dimensions={0}, use_global_device_ids=true | all-gather | bytes 152064 | tf_op jit(solution)/shard_map/all_gather | solution.py:22
  532.2 12.6 %left_product.14 = f32[1,4096]{1,0:T(1,128)S(1)} custom-call(f32[8,2,128]{2,1,0:T(2,128)S(1)} %bitcast.629, f32[2048,4096]{1,0:T(8,128)} %a_ref.31), custom_call_target="tpu_custom_call" | custom-call | tf_op jit(solution)/shard_map/left_product/pallas_call | solution.py:72
  545.7 30.5 %all-gather.34 = f32[8,1,4224]{2,1,0:T(1,128)S(1)} all-gather(f32[1,1,4224]{2,1,0:T(1,128)S(1)} %reshape.528), channel_id=17, replica_groups=mesh['prow'=8,'pcol'=4] {'prow'}, dimensions={0}, use_global_device_ids=true | all-gather | bytes 152064 | tf_op jit(solution)/shard_map/all_gather | solution.py:22
  583.8 12.4 %right_product.14 = f32[8,2,128]{2,1,0:T(2,128)S(1)} custom-call(f32[1,4096]{1,0:T(1,128)S(1)} %bitcast.575, f32[2048,4096]{1,0:T(8,128)} %a_ref.31), custom_call_target="tpu_custom_call" | custom-call | tf_op jit(solution)/shard_map/right_product/pallas_call | solution.py:104
  609.1 12.6 %left_product.15 = f32[1,4096]{1,0:T(1,128)S(1)} custom-call(f32[8,2,128]{2,1,0:T(2,128)S(1)} %bitcast.602, f32[2048,4096]{1,0:T(8,128)} %a_ref.31), custom_call_target="tpu_custom_call" | custom-call | tf_op jit(solution)/shard_map/left_product/pallas_call | solution.py:72
  622.7 30.5 %all-gather.36 = f32[8,1,4224]{2,1,0:T(1,128)S(1)} all-gather(f32[1,1,4224]{2,1,0:T(1,128)S(1)} %reshape.532), channel_id=19, replica_groups=mesh['prow'=8,'pcol'=4] {'prow'}, dimensions={0}, use_global_device_ids=true | all-gather | bytes 152064 | tf_op jit(solution)/shard_map/all_gather | solution.py:22
  660.9 12.4 %right_product.15 = f32[8,2,128]{2,1,0:T(2,128)S(1)} custom-call(f32[1,4096]{1,0:T(1,128)S(1)} %bitcast.571, f32[2048,4096]{1,0:T(8,128)} %a_ref.31), custom_call_target="tpu_custom_call" | custom-call | tf_op jit(solution)/shard_map/right_product/pallas_call | solution.py:104
  685.0 24.9 %convolution_subtract_fusion = f32[2048,4096]{1,0:T(8,128)} fusion(f32[2048,4096]{1,0:T(8,128)} %a_ref.31, bf16[96,2048]{1,0:T(8,128)(2,1)S(1)} %fusion.217, bf16[96,4096]{1,0:T(8,128)(2,1)S(1)} %constant_dynamic-update-slice_fusion.5), kind=kOutput, calls=%fused_computation | convolution fusion | flops 1619001344 | bytes 68288512 | tf_op jit(solution)/shard_map/dot_general | solution.py:246
  (388 shorter events, 187.2 us)
Async XLA Ops:
  609.1 75.6 %copy-start = (f32[1,1,2048]{2,1,0:T(1,128)S(1)}, f32[1,1,2048]{2,1,0:T(1,128)}, u32[]{:S(2)}) copy-start(f32[1,1,2048]{2,1,0:T(1,128)} %get-tuple-element.83) | copy-start | bytes 24580
